TPU v7x, 256 devices: a whole 4x4x8 slice. The times are simulated.
256 devices in a mesh: dp: 128 (over y, x_hi, z, core), mp: 2 (over x_lo).
Axes of the slice: x: 4 (x_hi: 2, x_lo: 2; x = x_hi * 2 + x_lo), y: 4, z: 8, core: 2. Of those that a mesh axis runs over, the one named last changes fastest.
Arguments:
- dino_tokens: bfloat16 [65536, 1024], P('dp', 'mp'), may hold values from -6 to 6
- siglip_tokens: bfloat16 [65536, 1152], P('dp', 'mp'), may hold values from -6 to 6
- dino_norm_one: float32 [1024], replicated, may hold values from 0.25 to 1.75
- dino_qkv: bfloat16 [1024, 3, 1024], P('dp', None, 'mp'), may hold values from -6.05625 to 6.05625
- dino_out: bfloat16 [1024, 1024], P('mp', 'dp'), may hold values from -0.1875 to 0.1875
- dino_norm_two: float32 [1024], replicated, may hold values from 0.25 to 1.75
- dino_up: bfloat16 [1024, 4096], P('dp', 'mp'), may hold values from -0.1875 to 0.1875
- dino_down: bfloat16 [4096, 1024], P('mp', 'dp'), may hold values from -0.09375 to 0.09375
- siglip_norm_one: float32 [1152], replicated, may hold values from 0.25 to 1.75
- siglip_qkv: bfloat16 [1152, 3, 1152], P('dp', None, 'mp'), may hold values from -5.709887 to 5.709887
- siglip_out: bfloat16 [1152, 1152], P('mp', 'dp'), may hold values from -0.1875 to 0.1875
- siglip_norm_two: float32 [1152], replicated, may hold values from 0.25 to 1.75
- siglip_up: bfloat16 [1152, 4304], P('dp', 'mp'), may hold values from -0.1875 to 0.1875
- siglip_down: bfloat16 [4304, 1152], P('mp', 'dp'), may hold values from -0.09375 to 0.09375
Outputs:
- dino_result: bfloat16 [65536, 1024], P('dp', 'mp')
- siglip_result: bfloat16 [65536, 1152], P('dp', 'mp')
All inputs are finite; a program needn't handle non-finite values.
Results may differ from a plain program's by a relative error of at most 0.012.
Values may be sent and summed in bfloat16 or wider, within the bound.
A program may use at most 128 MiB of HBM per device.

v0:
```python
import math
import jax
import jax.numpy as jnp
from jax import lax
from jax.sharding import PartitionSpec as P

HEADS = 16
PATCHES = 256
EPS = 1e-06


def from_everyone(shard, axis):
    size = lax.axis_size(axis)
    return lax.all_to_all(
        jnp.broadcast_to(shard[None], (size, *shard.shape)), axis, 0, 0, tiled=True
    )


def laid_out(pieces, dim):
    shape = list(pieces.shape[1:])
    shape[dim] *= pieces.shape[0]
    return jnp.moveaxis(pieces, 0, dim).reshape(shape)


def gathered_copies(shard, axis, dim):
    pieces = from_everyone(shard, axis)
    return laid_out(pieces, dim)


def split_up(shard, dim, size):
    shape = shard.shape
    pieces = shard.reshape(*shape[:dim], size, shape[dim] // size, *shape[dim + 1 :])
    return jnp.moveaxis(pieces, dim, 0)


def sum_at_owner(shard, axis, dim):
    pieces = split_up(shard, dim, lax.axis_size(axis))
    arrived = lax.all_to_all(pieces, axis, split_axis=0, concat_axis=0, tiled=True)
    return arrived.astype(jnp.float32).sum(axis=0)


def layer_norm(values, gain):
    values = values.astype(jnp.float32)
    center = values - jnp.mean(values, axis=-1, keepdims=True)
    spread = jnp.mean(center * center, axis=-1, keepdims=True)
    return (center * lax.rsqrt(spread + EPS) * gain).astype(jnp.bfloat16)


def encoder(tokens, norm_one, qkv_weight, out_weight, norm_two, up_weight, down_weight, approx):
    rows, local_width = tokens.shape
    whole = gathered_copies(tokens, "mp", 1)
    width = whole.shape[1]
    head_size = width // HEADS
    local_heads = qkv_weight.shape[2] // head_size
    scale = 1.0 / math.sqrt(head_size)
    normed = layer_norm(whole, norm_one)

    def fold_rows(source, piece):
        count = piece.shape[0]
        return jnp.dot(source, piece.reshape(count, -1), preferred_element_type=jnp.float32)

    qkv = fold_rows(normed, lax.all_gather(qkv_weight, "dp", axis=0, tiled=True))
    qkv = qkv.astype(jnp.bfloat16).reshape(rows // PATCHES, PATCHES, 3, local_heads, head_size)
    query = qkv[:, :, 0]
    keys = qkv[:, :, 1]
    values = qkv[:, :, 2]
    scores = jnp.einsum("fqhd,fkhd->fhqk", query, keys, preferred_element_type=jnp.float32) * scale
    top = jnp.max(scores, axis=-1, keepdims=True)
    expo = jnp.exp(scores - top)
    probs = (expo / jnp.sum(expo, axis=-1, keepdims=True)).astype(jnp.bfloat16)
    context = jnp.einsum("fhqk,fkhd->fqhd", probs, values, preferred_element_type=jnp.float32)
    context = context.astype(jnp.bfloat16).reshape(rows, local_heads * head_size)
    partial_attn = jnp.dot(
        context,
        lax.all_gather(out_weight, "dp", axis=1, tiled=True),
        preferred_element_type=jnp.float32,
    )
    share = sum_at_owner(partial_attn.astype(jnp.bfloat16), "mp", 1)
    middle = (tokens.astype(jnp.float32) + share).astype(jnp.bfloat16)
    middle_whole = gathered_copies(middle, "mp", 1)
    second = layer_norm(middle_whole, norm_two)
    raised = fold_rows(second, lax.all_gather(up_weight, "dp", axis=0, tiled=True))
    hidden = jax.nn.gelu(raised, approximate=approx).astype(jnp.bfloat16)
    partial_mlp = jnp.dot(
        hidden,
        lax.all_gather(down_weight, "dp", axis=1, tiled=True),
        preferred_element_type=jnp.float32,
    )
    mlp_part = sum_at_owner(partial_mlp.astype(jnp.bfloat16), "mp", 1)
    return (middle.astype(jnp.float32) + mlp_part).astype(jnp.bfloat16)


def local(
    dino_tokens,
    siglip_tokens,
    dino_norm_one,
    dino_qkv,
    dino_out,
    dino_norm_two,
    dino_up,
    dino_down,
    siglip_norm_one,
    siglip_qkv,
    siglip_out,
    siglip_norm_two,
    siglip_up,
    siglip_down,
):
    dino_result = encoder(
        dino_tokens, dino_norm_one, dino_qkv, dino_out, dino_norm_two, dino_up, dino_down, False
    )
    siglip_result = encoder(
        siglip_tokens,
        siglip_norm_one,
        siglip_qkv,
        siglip_out,
        siglip_norm_two,
        siglip_up,
        siglip_down,
        True,
    )
    return (dino_result, siglip_result)


def solution(mesh):
    in_specs = (
        P("dp", "mp"),
        P("dp", "mp"),
        P(),
        P("dp", None, "mp"),
        P("mp", "dp"),
        P(),
        P("dp", "mp"),
        P("mp", "dp"),
        P(),
        P("dp", None, "mp"),
        P("mp", "dp"),
        P(),
        P("dp", "mp"),
        P("mp", "dp"),
    )
    out_specs = (P("dp", "mp"), P("dp", "mp"))
    return jax.shard_map(local, mesh=mesh, in_specs=in_specs, out_specs=out_specs, check_vma=False)
```

profile of v0, /device:TPU:1, one launch (start us, length us, event | category | flops | bytes accessed | tf_op | source)
XLA Modules:
  0.0 1024.6 jit_solution(13799758242859776503)
XLA Ops:
  7.2 0.7 all-gather.12.cloned.1.call-update
  8.0 0.7 all-gather.14.cloned.1.call-update
  8.7 0.7 all-gather.22.cloned.1.call-update
  11.2 0.7 all-gather.24.cloned.1.call-update
  11.9 1.3 copy.43
  13.2 1.1 broadcast_in_dim.8
  14.2 3.6 all-to-all-start
  17.8 11.6 %all-to-all-done = bf16[2,512,512]{1,2,0:T(8,128)(2,1)S(1)} async-done(((bf16[2,512,512]{1,2,0:T(8,128)(2,1)}), bf16[2,512,512]{1,2,0:T(8,128)(2,1)S(1)}, u32[]{:S(2)}, u32[]{:S(2)}) %all-to-all-start) | async-done | bytes 1048608 | tf_op jit(solution)/shard_map/all_to_all | solution.py:14
  29.4 1.1 broadcast_in_dim.10
  30.6 3.6 all-to-all-start.4
  34.7 1.3 fusion.43
  36.1 90.8 %all-gather.12.cloned.1.call-done = bf16[1024,3,512]{2,0,1:T(8,128)(2,1)} async-done(((bf16[8,3,512]{2,0,1:T(8,128)(2,1)}), bf16[1024,3,512]{2,0,1:T(8,128)(2,1)}) %all-gather.12.cloned.1.call-update) | async-done | bytes 3145744 | tf_op jit(solution)/shard_map/all_gather | solution.py:62
  126.8 4.7 copy.44
  131.5 4.1 convolution_convert_fusion.2
  135.6 3.2 reshape.172
  138.7 3.1 fusion.101
  141.8 2.5 copy.67
  144.3 1.4 copy.68
  145.7 0.6 copy.66
  146.3 2.0 fusion.61
  148.3 3.2 fusion.103
  152.7 78.1 %all-gather.14.cloned.1.call-done = bf16[512,1024]{0,1:T(8,128)(2,1)} async-done(((bf16[512,8]{0,1:T(8,128)(2,1)}), bf16[512,1024]{0,1:T(8,128)(2,1)}) %all-gather.14.cloned.1.call-update) | async-done | bytes 1048592 | tf_op jit(solution)/shard_map/all_gather | solution.py:75
  230.8 2.0 convolution_convert_fusion.4
  232.8 1.1 copy.85
  233.9 3.6 all-to-all-start.1
  237.5 0.7 all-gather.26.cloned.1.call-update
  238.5 12.6 %all-to-all-done.1 = bf16[2,512,512]{2,1,0:T(8,128)(2,1)S(1)} async-done(((bf16[2,512,512]{2,1,0:T(8,128)(2,1)}), bf16[2,512,512]{2,1,0:T(8,128)(2,1)S(1)}, u32[]{:S(2)}, u32[]{:S(2)}) %all-to-all-start.1) | async-done | bytes 1048608 | tf_op jit(solution)/shard_map/all_to_all | solution.py:38
  251.7 1.1 broadcast_in_dim.9
  252.8 4.0 all-to-all-start.2
  257.2 1.4 fusion.32
  258.6 91.0 %all-gather.22.cloned.1.call-done = bf16[128,9,576]{2,1,0:T(8,128)(2,1)} async-done(((bf16[1,9,576]{2,1,0:T(8,128)(2,1)}), bf16[128,9,576]{2,1,0:T(8,128)(2,1)}) %all-gather.22.cloned.1.call-update) | async-done | bytes 1327120 | tf_op jit(solution)/shard_map/all_gather | solution.py:75
  349.6 4.1 reshape.167
  353.9 118.7 %all-gather.20.cloned.1.call-done = bf16[1152,3,576]{2,1,0:T(4,128)(2,1)} async-done(((bf16[9,3,576]{2,1,0:T(4,128)(2,1)}), bf16[1152,3,576]{2,1,0:T(4,128)(2,1)}) %all-gather.20.cloned.1.call-update) | async-done | bytes 3981328 | tf_op jit(solution)/shard_map/all_gather | solution.py:62
  472.6 11.3 %copy.54 = bf16[1152,3,576]{0,2,1:T(8,128)(2,1)} copy(bf16[1152,3,576]{2,1,0:T(4,128)(2,1)} %all-gather.20.cloned.1.call-done) | data formatting | bytes 7962624 | tf_op jit(solution)/shard_map/all_gather | solution.py:62
  484.0 5.8 convolution_convert_fusion
  489.8 4.8 reshape.160
  494.6 2.6 fusion.102
  497.2 0.7 fusion.60
  498.0 3.2 fusion.104
  501.7 0.6 copy.59
  502.6 1.3 convolution_convert_fusion.1
  503.9 1.5 copy.60
  505.3 3.7 all-to-all-start.5
  509.4 1.3 fusion.46
  510.7 13.2 %all-to-all-done.5 = bf16[2,512,576]{1,2,0:T(8,128)(2,1)S(1)} async-done(((bf16[2,512,576]{1,2,0:T(8,128)(2,1)}), bf16[2,512,576]{1,2,0:T(8,128)(2,1)S(1)}, u32[]{:S(2)}, u32[]{:S(2)}) %all-to-all-start.5) | async-done | bytes 1179680 | tf_op jit(solution)/shard_map/all_to_all | solution.py:38
  524.3 1.1 broadcast_in_dim.11
  525.5 3.8 all-to-all-start.6
  529.3 63.4 %all-gather.16.cloned.1.call-done = bf16[1024,2048]{1,0:T(8,128)(2,1)} async-done(((bf16[8,2048]{1,0:T(8,128)(2,1)}), bf16[1024,2048]{1,0:T(8,128)(2,1)}) %all-gather.16.cloned.1.call-update) | async-done | bytes 4194320 | tf_op jit(solution)/shard_map/all_gather | solution.py:82
  592.7 120.0 %all-gather.18.cloned.1.call-done = bf16[2048,1024]{0,1:T(8,128)(2,1)} async-done(((bf16[2048,8]{0,1:T(8,128)(2,1)}), bf16[2048,1024]{0,1:T(8,128)(2,1)}) %all-gather.18.cloned.1.call-update) | async-done | bytes 4194320 | tf_op jit(solution)/shard_map/all_gather | solution.py:86
  712.7 17.9 %fusion.53 = bf16[512,1024]{1,0:T(8,128)(2,1)} fusion(bf16[2048,1024]{0,1:T(8,128)(2,1)} %all-gather.18.cloned.1.call-done, bf16[512,1024]{0,1:T(8,128)(2,1)} %fusion.46, bf16[1024,2048]{1,0:T(8,128)(2,1)} %all-gather.16.cloned.1.call-done), kind=kOutput, calls=%fused_computation.79 | convolution fusion | flops 4363649024 | bytes 10485760 | tf_op jit(solution)/shard_map/dot_general | solution.py:84
  730.7 2.3 copy.84
  733.0 4.5 all-to-all-start.3
  738.1 1.4 fusion.35
  739.5 103.9 %all-gather.24.cloned.1.call-done = bf16[128,9,2152]{2,1,0:T(8,128)(2,1)} async-done(((bf16[1,9,2152]{2,1,0:T(8,128)(2,1)}), bf16[128,9,2152]{2,1,0:T(8,128)(2,1)}) %all-gather.24.cloned.1.call-update) | async-done | bytes 4958224 | tf_op jit(solution)/shard_map/all_gather | solution.py:82
  843.4 9.1 reshape.169
  852.5 121.5 %all-gather.26.cloned.1.call-done = bf16[128,9,2152]{2,1,0:T(8,128)(2,1)} async-done(((bf16[1,9,2152]{2,1,0:T(8,128)(2,1)}), bf16[128,9,2152]{2,1,0:T(8,128)(2,1)}) %all-gather.26.cloned.1.call-update) | async-done | bytes 4958224 | tf_op jit(solution)/shard_map/all_gather | solution.py:86
  974.1 9.1 reshape.171
  983.2 12.2 %convolution_convert_fusion.3 = bf16[512,1152]{1,0:T(8,128)(2,1)} fusion(bf16[1152,2152]{1,0:T(8,128)(2,1)} %reshape.171, bf16[512,1152]{0,1:T(8,128)(2,1)S(1)} %copy-done.5, bf16[1152,2152]{1,0:T(8,128)(2,1)} %reshape.169), kind=kOutput, calls=%fused_computation.41 | convolution fusion | flops 5087711232 | bytes 12275712 | tf_op jit(solution)/shard_map/dot_general | solution.py:84
  995.4 2.4 copy.61
  997.8 3.6 all-to-all-start.7
  1001.4 1.5 convert_reduce_fusion.4
  1002.9 1.0 add_convert_fusion.2
  1003.9 12.4 %all-to-all-done.7 = bf16[2,512,576]{1,2,0:T(8,128)(2,1)S(1)} async-done(((bf16[2,512,576]{1,2,0:T(8,128)(2,1)}), bf16[2,512,576]{1,2,0:T(8,128)(2,1)S(1)}, u32[]{:S(2)}, u32[]{:S(2)}) %all-to-all-start.7) | async-done | bytes 1179680 | tf_op jit(solution)/shard_map/all_to_all | solution.py:38
  1016.5 1.0 add_convert_fusion
  (64 shorter events, 7.4 us)
Async XLA Ops:
  7.2 10.7 %copy-start.9 = (f32[1024]{0:T(1024)S(1)}, f32[1024]{0:T(1024)}, u32[]{:S(2)}) copy-start(f32[1024]{0:T(1024)} %param.16) | copy-start | bytes 12292
  7.2 22.3 %copy-start = (bf16[512,576]{0,1:T(8,128)(2,1)S(1)}, bf16[512,576]{0,1:T(8,128)(2,1)}, u32[]{:S(2)}) copy-start(bf16[512,576]{0,1:T(8,128)(2,1)} %param.15) | copy-start | bytes 1769476
  7.2 119.6 %all-gather.12.cloned.1.call-start = ((), (), s32[]{:S(2)}) async-start(), calls=%async_computation.8 | async-start | bytes 3170304 | tf_op jit(solution)/shard_map/all_gather | solution.py:62
  7.9 222.9 %all-gather.14.cloned.1.call-start = ((), (), s32[]{:S(2)}) async-start(), calls=%async_computation.9 | async-start | bytes 1056768 | tf_op jit(solution)/shard_map/all_gather | solution.py:75
  8.7 340.9 %all-gather.22.cloned.1.call-start = ((), (), s32[]{:S(2)}) async-start(), calls=%async_computation.13 | async-start | bytes 2641920 | tf_op jit(solution)/shard_map/all_gather | solution.py:75
  9.4 463.2 %all-gather.20.cloned.1.call-start = ((), (), s32[]{:S(2)}) async-start(), calls=%async_computation.12 | async-start | bytes 5944320 | tf_op jit(solution)/shard_map/all_gather | solution.py:62
  10.0 582.7 %all-gather.16.cloned.1.call-start = ((), (), s32[]{:S(2)}) async-start(), calls=%async_computation.10 | async-start | bytes 4227072 | tf_op jit(solution)/shard_map/all_gather | solution.py:82
  10.6 702.2 %all-gather.18.cloned.1.call-start = ((), (), s32[]{:S(2)}) async-start(), calls=%async_computation.11 | async-start | bytes 4227072 | tf_op jit(solution)/shard_map/all_gather | solution.py:86
  11.1 832.3 %all-gather.24.cloned.1.call-start = ((), (), s32[]{:S(2)}) async-start(), calls=%async_computation.14 | async-start | bytes 8982528 | tf_op jit(solution)/shard_map/all_gather | solution.py:82
  14.2 15.2 %all-to-all-start = ((bf16[2,512,512]{1,2,0:T(8,128)(2,1)}), bf16[2,512,512]{1,2,0:T(8,128)(2,1)S(1)}, u32[]{:S(2)}, u32[]{:S(2)}) async-start(bf16[2,512,512]{1,2,0:T(8,128)(2,1)} %broadcast_in_dim.8), calls=%async_computation | async-start | bytes 2097152 | tf_op jit(solution)/shard_map/all_to_all | solution.py:14
  30.6 203.3 %all-to-all-start.4 = ((bf16[2,512,576]{1,2,0:T(8,128)(2,1)}), bf16[2,512,576]{1,2,0:T(8,128)(2,1)S(1)}, u32[]{:S(2)}, u32[]{:S(2)}) async-start(bf16[2,512,576]{1,2,0:T(8,128)(2,1)} %broadcast_in_dim.10), calls=%async_computation.4 | async-start | bytes 2359296 | tf_op jit(solution)/shard_map/all_to_all | solution.py:14
  152.6 85.7 %copy-start.7 = (f32[1152]{0:T(1024)S(1)}, f32[1152]{0:T(1024)}, u32[]{:S(2)}) copy-start(f32[1152]{0:T(1024)} %param.22) | copy-start | bytes 13828
  232.8 18.5 %copy-start.2 = (bf16[512,512]{1,0:T(8,128)(2,1)S(1)}, bf16[512,512]{1,0:T(8,128)(2,1)}, u32[]{:S(2)}) copy-start(bf16[512,512]{1,0:T(8,128)(2,1)} %param.14) | copy-start | bytes 1572868
  233.9 17.2 %all-to-all-start.1 = ((bf16[2,512,512]{2,1,0:T(8,128)(2,1)}), bf16[2,512,512]{2,1,0:T(8,128)(2,1)S(1)}, u32[]{:S(2)}, u32[]{:S(2)}) async-start(bf16[2,512,512]{2,1,0:T(8,128)(2,1)} %bitcast.102), calls=%async_computation.1 | async-start | bytes 2097152 | tf_op jit(solution)/shard_map/all_to_all | solution.py:38
  237.5 736.6 %all-gather.26.cloned.1.call-start = ((), (), s32[]{:S(2)}) async-start(), calls=%async_computation.15 | async-start | bytes 8982528 | tf_op jit(solution)/shard_map/all_gather | solution.py:86
  252.8 100.9 %all-to-all-start.2 = ((bf16[2,512,512]{1,2,0:T(8,128)(2,1)}), bf16[2,512,512]{1,2,0:T(8,128)(2,1)S(1)}, u32[]{:S(2)}, u32[]{:S(2)}) async-start(bf16[2,512,512]{1,2,0:T(8,128)(2,1)} %broadcast_in_dim.9), calls=%async_computation.2 | async-start | bytes 2097152 | tf_op jit(solution)/shard_map/all_to_all | solution.py:14
  353.9 130.0 %copy-start.4 = (bf16[2,512,576]{1,2,0:T(8,128)(2,1)S(1)}, bf16[2,512,576]{1,2,0:T(8,128)(2,1)}, u32[]{:S(2)}) copy-start(bf16[2,512,576]{1,2,0:T(8,128)(2,1)} %fusion.32) | copy-start | bytes 3538948
  501.2 1.4 copy-start.3
  502.6 6.8 copy-start.8
  505.3 18.8 %copy-start.1 = (bf16[512,576]{0,1:T(8,128)(2,1)S(1)}, bf16[512,576]{0,1:T(8,128)(2,1)}, u32[]{:S(2)}) copy-start(bf16[512,576]{0,1:T(8,128)(2,1)} %param.15) | copy-start | bytes 1769476
  505.3 18.6 %all-to-all-start.5 = ((bf16[2,512,576]{1,2,0:T(8,128)(2,1)}), bf16[2,512,576]{1,2,0:T(8,128)(2,1)S(1)}, u32[]{:S(2)}, u32[]{:S(2)}) async-start(bf16[2,512,576]{1,2,0:T(8,128)(2,1)} %bitcast.21), calls=%async_computation.5 | async-start | bytes 2359296 | tf_op jit(solution)/shard_map/all_to_all | solution.py:38
  525.5 207.5 %all-to-all-start.6 = ((bf16[2,512,576]{1,2,0:T(8,128)(2,1)}), bf16[2,512,576]{1,2,0:T(8,128)(2,1)S(1)}, u32[]{:S(2)}, u32[]{:S(2)}) async-start(bf16[2,512,576]{1,2,0:T(8,128)(2,1)} %broadcast_in_dim.11), calls=%async_computation.6 | async-start | bytes 2359296 | tf_op jit(solution)/shard_map/all_to_all | solution.py:14
  730.7 7.4 copy-start.6
  733.0 264.8 %all-to-all-start.3 = ((bf16[2,512,512]{2,1,0:T(8,128)(2,1)}), bf16[2,512,512]{2,1,0:T(8,128)(2,1)}, u32[]{:S(2)}, u32[]{:S(2)}) async-start(bf16[2,512,512]{2,1,0:T(8,128)(2,1)} %bitcast.103), calls=%async_computation.3 | async-start | bytes 2097152 | tf_op jit(solution)/shard_map/all_to_all | solution.py:38
  852.5 130.7 %copy-start.5 = (bf16[512,1152]{0,1:T(8,128)(2,1)S(1)}, bf16[512,1152]{0,1:T(8,128)(2,1)}, u32[]{:S(2)}) copy-start(bf16[512,1152]{0,1:T(8,128)(2,1)} %fusion.35) | copy-start | bytes 3538948
  997.8 18.4 %all-to-all-start.7 = ((bf16[2,512,576]{1,2,0:T(8,128)(2,1)}), bf16[2,512,576]{1,2,0:T(8,128)(2,1)S(1)}, u32[]{:S(2)}, u32[]{:S(2)}) async-start(bf16[2,512,576]{1,2,0:T(8,128)(2,1)} %bitcast.28), calls=%async_computation.7 | async-start | bytes 2359296 | tf_op jit(solution)/shard_map/all_to_all | solution.py:38
Sparse Core Ops, SparseCore 0:
  11.8 114.9 all-gather.11
  130.6 100.1 all-gather.13
  234.4 115.1 all-gather.21
  353.1 119.4 all-gather.19
  476.0 116.5 all-gather.15
  596.1 116.5 all-gather.17
  716.3 127.0 all-gather.23
  847.0 127.0 all-gather.25
where the time goes:
time: 1030 us; the launch traced here: 1020 us
  waiting for transfers between devices  842 us (82%)
  local copies, waits for them, and re-layouts  71.3 us (7%)
  matrix products  46.9 us (5%)
  starting transfers between devices  30.7 us (3%)
  other arithmetic  18.8 us (2%)
  between operations  14.7 us (1%)
    all_gather x2, waiting for transfers between devices, encoder(): lax.all_gather(down_weight, 'dp', axis=1, tiled=True)  242 us
    all_gather x2, waiting for transfers between devices, encoder(): lax.all_gather(qkv_weight, 'dp', axis=0, tiled=True)  209 us
    all_gather x2, waiting for transfers between devices, encoder(): lax.all_gather(out_weight, 'dp', axis=1, tiled=True)  169 us
    all_gather x2, waiting for transfers between devices, encoder(): lax.all_gather(up_weight, 'dp', axis=0, tiled=True)  167 us
    all_to_all x4, waiting for transfers between devices, sum_at_owner(): lax.all_to_all(pieces, axis, split_axis=0, concat_axis=0, tiled=True)  38.1 us
    dot_general x2, matrix products, encoder(): jnp.dot(hidden, lax.all_gather(down_weight, 'dp', axis=1, tiled=True), pr...  30.1 us
    unnamed x29, local copies, waits for them, and re-layouts  28.5 us
  transfers between devices with their start and end apart: 16, of which 12 were waited for; matrix products, arithmetic and copies ran while one was open for 13% of the time, Pallas kernels for 0%

commit v1 on v0

--- a/solution.py
+++ b/solution.py
@@ -83,7 +83,9 @@
     hidden = jax.nn.gelu(raised, approximate=approx).astype(jnp.bfloat16)
     partial_mlp = jnp.dot(
         hidden,
-        lax.all_gather(down_weight, "dp", axis=1, tiled=True),
+        jnp.concatenate(
+            lax.all_to_all(jnp.stack([down_weight] * lax.axis_size("dp")), "dp", 0, 0), axis=1
+        ),
         preferred_element_type=jnp.float32,
     )
     mlp_part = sum_at_owner(partial_mlp.astype(jnp.bfloat16), "mp", 1)

time: 1030 us -> 965 us (0.937)
  waiting for transfers between devices: 842 us -> 719 us
  blocking collectives: 0 us -> 33.3 us
  starting transfers between devices: 30.7 us -> 48.5 us
    all_to_all x0 -> x2, waiting for transfers between devices: none -> 298 us  [encoder(): lax.all_to_all(jnp.stack([down_weight] * lax.axis_size('dp')), 'dp', 0, 0)]
    all_gather x2 -> x0, waiting for transfers between devices: 242 us -> none  [encoder(): lax.all_gather(down_weight, 'dp', axis=1, tiled=True)]
    all_gather x2, waiting for transfers between devices: 167 us -> 0.01 us  [encoder(): lax.all_gather(up_weight, 'dp', axis=0, tiled=True)]
    all_to_all x0 -> x2, blocking collectives: none -> 33.3 us  [the longest x1 17.3 us: sum_at_owner(): lax.all_to_all(pieces, axis, split_axis=0, concat_axis=0, tiled=True)]
    all_to_all x4 -> x3, waiting for transfers between devices: 38.1 us -> 11.2 us  [sum_at_owner(): lax.all_to_all(pieces, axis, split_axis=0, concat_axis=0, tiled=True)]
    all_to_all x0 -> x2, starting transfers between devices: none -> 26.1 us  [encoder(): lax.all_to_all(jnp.stack([down_weight] * lax.axis_size('dp')), 'dp', 0, 0)]
    all_gather x2, waiting for transfers between devices: 169 us -> 189 us  [encoder(): lax.all_gather(out_weight, 'dp', axis=1, tiled=True)]
    all_gather x2, waiting for transfers between devices: 209 us -> 196 us  [encoder(): lax.all_gather(qkv_weight, 'dp', axis=0, tiled=True)]
  transfers between devices with their start and end apart: 16 -> 14, of which waited for: 12 -> 9; matrix products, arithmetic and copies ran while one was open for 13% -> 14% of each run, Pallas kernels for 0% -> 0%
where the time goes in v1:
time: 965 us; the launch traced here: 953 us
  waiting for transfers between devices  719 us (75%)
  local copies, waits for them, and re-layouts  73.3 us (8%)
  starting transfers between devices  48.5 us (5%)
  matrix products  45.8 us (5%)
  blocking collectives  33.3 us (3%)
  other arithmetic  18.7 us (2%)
  between operations  14.7 us (2%)
    all_to_all x2, waiting for transfers between devices, encoder(): lax.all_to_all(jnp.stack([down_weight] * lax.axis_size('dp')), 'dp', 0, 0)  298 us
    all_gather x2, waiting for transfers between devices, encoder(): lax.all_gather(qkv_weight, 'dp', axis=0, tiled=True)  196 us
    all_gather x2, waiting for transfers between devices, encoder(): lax.all_gather(out_weight, 'dp', axis=1, tiled=True)  189 us
    dot_general x2, matrix products, encoder(): jnp.dot(hidden, jnp.concatenate(lax.all_to_all(jnp.stack([down_weight] *...  29 us
    all_to_all x2, starting transfers between devices, encoder(): lax.all_to_all(jnp.stack([down_weight] * lax.axis_size('dp')), 'dp', 0, 0)  26.1 us
    all_to_all x3, waiting for transfers between devices, from_everyone(): lax.all_to_all(jnp.broadcast_to(shard[None], (size, *shard.shape)), axis,...  21.3 us
    unnamed x38, local copies, waits for them, and re-layouts  20.4 us
  transfers between devices with their start and end apart: 14, of which 9 were waited for; matrix products, arithmetic and copies ran while one was open for 14% of the time, Pallas kernels for 0%

profile of v1, /device:TPU:1, one launch (start us, length us, event | category | flops | bytes accessed | tf_op | source)
XLA Modules:
  0.0 953.4 jit_solution(9698022035935879585)
XLA Ops:
  7.2 0.7 all-gather.9.cloned.1.call-update
  8.0 0.7 all-gather.11.cloned.1.call-update
  8.7 0.7 all-gather.17.cloned.1.call-update
  10.0 1.3 copy.45
  11.2 1.0 broadcast_in_dim.8
  12.3 3.6 all-to-all-start
  16.0 11.5 %all-to-all-done = bf16[2,512,512]{1,2,0:T(8,128)(2,1)S(1)} async-done(((bf16[2,512,512]{1,2,0:T(8,128)(2,1)}), bf16[2,512,512]{1,2,0:T(8,128)(2,1)S(1)}, u32[]{:S(2)}, u32[]{:S(2)}) %all-to-all-start) | async-done | bytes 1048608 | tf_op jit(solution)/shard_map/all_to_all | solution.py:14
  27.5 1.1 broadcast_in_dim.10
  28.6 3.6 all-to-all-start.5
  32.8 1.3 fusion.46
  34.1 9.7 %all-to-all-done.5 = bf16[2,512,576]{1,2,0:T(8,128)(2,1)S(1)} async-done(((bf16[2,512,576]{1,2,0:T(8,128)(2,1)}), bf16[2,512,576]{1,2,0:T(8,128)(2,1)S(1)}, u32[]{:S(2)}, u32[]{:S(2)}) %all-to-all-start.5) | async-done | bytes 1179680 | tf_op jit(solution)/shard_map/all_to_all | solution.py:14
  44.1 82.8 %all-gather.9.cloned.1.call-done = bf16[1024,3,512]{2,0,1:T(8,128)(2,1)} async-done(((bf16[8,3,512]{2,0,1:T(8,128)(2,1)}), bf16[1024,3,512]{2,0,1:T(8,128)(2,1)}) %all-gather.9.cloned.1.call-update) | async-done | bytes 3145744 | tf_op jit(solution)/shard_map/all_gather | solution.py:62
  126.8 4.7 copy.46
  131.5 4.1 convolution_convert_fusion.2
  135.6 3.2 reshape.190
  138.8 3.1 fusion.134
  141.8 2.5 copy.69
  144.3 1.4 copy.70
  145.7 0.6 copy.68
  146.3 2.0 fusion.94
  148.3 3.2 fusion.136
  152.0 0.5 copy.52
  152.7 78.2 %all-gather.11.cloned.1.call-done = bf16[512,1024]{0,1:T(8,128)(2,1)} async-done(((bf16[512,8]{0,1:T(8,128)(2,1)}), bf16[512,1024]{0,1:T(8,128)(2,1)}) %all-gather.11.cloned.1.call-update) | async-done | bytes 1048592 | tf_op jit(solution)/shard_map/all_gather | solution.py:75
  230.8 2.0 convolution_convert_fusion.4
  232.8 1.1 copy.87
  233.9 3.6 all-to-all-start.1
  237.8 1.4 fusion.34
  239.2 110.4 %all-gather.17.cloned.1.call-done = bf16[128,9,576]{2,1,0:T(8,128)(2,1)} async-done(((bf16[1,9,576]{2,1,0:T(8,128)(2,1)}), bf16[128,9,576]{2,1,0:T(8,128)(2,1)}) %all-gather.17.cloned.1.call-update) | async-done | bytes 1327120 | tf_op jit(solution)/shard_map/all_gather | solution.py:75
  349.6 4.1 reshape.187
  354.3 1.0 broadcast_in_dim.9
  355.3 3.8 all-to-all-start.2
  359.1 113.5 %all-gather.15.cloned.1.call-done = bf16[1152,3,576]{2,1,0:T(4,128)(2,1)} async-done(((bf16[9,3,576]{2,1,0:T(4,128)(2,1)}), bf16[1152,3,576]{2,1,0:T(4,128)(2,1)}) %all-gather.15.cloned.1.call-update) | async-done | bytes 3981328 | tf_op jit(solution)/shard_map/all_gather | solution.py:62
  472.7 11.3 %copy.56 = bf16[1152,3,576]{0,2,1:T(8,128)(2,1)} copy(bf16[1152,3,576]{2,1,0:T(4,128)(2,1)} %all-gather.15.cloned.1.call-done) | data formatting | bytes 7962624 | tf_op jit(solution)/shard_map/all_gather | solution.py:62
  484.0 5.8 convolution_convert_fusion
  489.8 3.9 reshape.178
  493.7 1.2 fusion.135
  495.0 0.8 fusion.93
  495.7 3.2 fusion.137
  499.4 0.6 copy.61
  500.4 1.3 convolution_convert_fusion.1
  501.6 0.6 copy.62
  502.3 17.3 %all_to_all.50 = bf16[2,512,576]{1,2,0:T(8,128)(2,1)S(1)} all-to-all(bf16[2,512,576]{1,2,0:T(8,128)(2,1)S(1)} %bitcast.109), channel_id=1, replica_groups=mesh['dp'=128,'mp'=2] {'mp'}, dimensions={0} | all-to-all | bytes 2359296 | tf_op jit(solution)/shard_map/all_to_all | solution.py:38
  519.5 2.5 stack.4
  522.0 10.4 %all-to-all-start.3 = ((bf16[128,2048,8]{1,2,0:T(8,128)(2,1)}), bf16[128,2048,8]{1,2,0:T(8,128)(2,1)}, u32[]{:S(2)}, u32[]{:S(2)}) async-start(bf16[128,2048,8]{1,2,0:T(8,128)(2,1)} %stack.4), calls=%async_computation.3 | async-start | bytes 8388608 | tf_op jit(solution)/shard_map/all_to_all | solution.py:87
  533.5 99.6 %all-to-all-done.3 = bf16[128,2048,8]{1,2,0:T(8,128)(2,1)} async-done(((bf16[128,2048,8]{1,2,0:T(8,128)(2,1)}), bf16[128,2048,8]{1,2,0:T(8,128)(2,1)}, u32[]{:S(2)}, u32[]{:S(2)}) %all-to-all-start.3) | async-done | bytes 4194336 | tf_op jit(solution)/shard_map/all_to_all | solution.py:87
  633.1 16.0 %all_to_all.51 = bf16[2,512,576]{1,2,0:T(8,128)(2,1)S(1)} all-to-all(bf16[2,512,576]{1,2,0:T(8,128)(2,1)S(1)} %broadcast_in_dim.11), channel_id=1, replica_groups=mesh['dp'=128,'mp'=2] {'mp'}, dimensions={0} | all-to-all | bytes 2359296 | tf_op jit(solution)/shard_map/all_to_all | solution.py:14
  649.1 4.1 stack.5
  653.2 15.7 %all-to-all-start.8 = ((bf16[128,2152,9]{1,2,0:T(8,128)(2,1)}), bf16[128,2152,9]{1,2,0:T(8,128)(2,1)}, u32[]{:S(2)}, u32[]{:S(2)}) async-start(bf16[128,2152,9]{1,2,0:T(8,128)(2,1)} %stack.5), calls=%async_computation.8 | async-start | bytes 17825792 | tf_op jit(solution)/shard_map/all_to_all | solution.py:87
  670.1 1.3 fusion.49
  671.4 16.9 %fusion.84 = bf16[512,1024]{1,0:T(8,128)(2,1)S(1)} fusion(bf16[128,2048,8]{1,2,0:T(8,128)(2,1)} %all-to-all-done.3, bf16[512,1024]{0,1:T(8,128)(2,1)} %fusion.49, bf16[1024,2048]{1,0:T(8,128)(2,1)} %all-gather.13.cloned.1.call-done), kind=kOutput, calls=%fused_computation.111 | convolution fusion | flops 4363649024 | bytes 10485760 | tf_op jit(solution)/shard_map/dot_general | solution.py:84
  688.3 1.1 copy.86
  690.0 1.4 fusion.37
  691.4 198.9 %all-to-all-done.8 = bf16[128,2152,9]{1,2,0:T(8,128)(2,1)} async-done(((bf16[128,2152,9]{1,2,0:T(8,128)(2,1)}), bf16[128,2152,9]{1,2,0:T(8,128)(2,1)}, u32[]{:S(2)}, u32[]{:S(2)}) %all-to-all-start.8) | async-done | bytes 4958240 | tf_op jit(solution)/shard_map/all_to_all | solution.py:87
  890.3 3.6 all-to-all-start.4
  893.9 9.1 reshape.182
  903.0 9.1 reshape.189
  912.2 12.1 %convolution_convert_fusion.3 = bf16[512,1152]{1,0:T(8,128)(2,1)} fusion(bf16[2152,1152]{0,1:T(8,128)(2,1)} %reshape.182, bf16[512,1152]{0,1:T(8,128)(2,1)S(1)} %copy-done.8, bf16[1152,2152]{1,0:T(8,128)(2,1)} %reshape.189), kind=kOutput, calls=%fused_computation.43 | convolution fusion | flops 5087711232 | bytes 12275712 | tf_op jit(solution)/shard_map/dot_general | solution.py:84
  924.3 2.5 copy.63
  926.8 1.0 copy-done.2
  927.8 3.6 all-to-all-start.9
  931.4 1.5 convert_reduce_fusion.4
  932.9 1.0 add_convert_fusion.2
  933.9 11.2 %all-to-all-done.9 = bf16[2,512,576]{1,2,0:T(8,128)(2,1)S(1)} async-done(((bf16[2,512,576]{1,2,0:T(8,128)(2,1)}), bf16[2,512,576]{1,2,0:T(8,128)(2,1)S(1)}, u32[]{:S(2)}, u32[]{:S(2)}) %all-to-all-start.9) | async-done | bytes 1179680 | tf_op jit(solution)/shard_map/all_to_all | solution.py:38
  945.3 1.0 add_convert_fusion
  (72 shorter events, 6.9 us)
Async XLA Ops:
  7.2 8.7 copy-start.12
  7.2 8.8 copy-start.14
  7.2 20.3 %copy-start.3 = (bf16[512,576]{0,1:T(8,128)(2,1)S(1)}, bf16[512,576]{0,1:T(8,128)(2,1)}, u32[]{:S(2)}) copy-start(bf16[512,576]{0,1:T(8,128)(2,1)} %param.15) | copy-start | bytes 1769476
  7.2 119.6 %all-gather.9.cloned.1.call-start = ((), (), s32[]{:S(2)}) async-start(), calls=%async_computation.10 | async-start | bytes 3170304 | tf_op jit(solution)/shard_map/all_gather | solution.py:62
  7.9 222.9 %all-gather.11.cloned.1.call-start = ((), (), s32[]{:S(2)}) async-start(), calls=%async_computation.11 | async-start | bytes 1056768 | tf_op jit(solution)/shard_map/all_gather | solution.py:75
  8.7 341.0 %all-gather.17.cloned.1.call-start = ((), (), s32[]{:S(2)}) async-start(), calls=%async_computation.14 | async-start | bytes 2641920 | tf_op jit(solution)/shard_map/all_gather | solution.py:75
  9.4 463.2 %all-gather.15.cloned.1.call-start = ((), (), s32[]{:S(2)}) async-start(), calls=%async_computation.13 | async-start | bytes 5944320 | tf_op jit(solution)/shard_map/all_gather | solution.py:62
  12.3 15.2 %all-to-all-start = ((bf16[2,512,512]{1,2,0:T(8,128)(2,1)}), bf16[2,512,512]{1,2,0:T(8,128)(2,1)S(1)}, u32[]{:S(2)}, u32[]{:S(2)}) async-start(bf16[2,512,512]{1,2,0:T(8,128)(2,1)} %broadcast_in_dim.8), calls=%async_computation | async-start | bytes 2097152 | tf_op jit(solution)/shard_map/all_to_all | solution.py:14
  28.6 15.2 %all-to-all-start.5 = ((bf16[2,512,576]{1,2,0:T(8,128)(2,1)}), bf16[2,512,576]{1,2,0:T(8,128)(2,1)S(1)}, u32[]{:S(2)}, u32[]{:S(2)}) async-start(bf16[2,512,576]{1,2,0:T(8,128)(2,1)} %broadcast_in_dim.10), calls=%async_computation.5 | async-start | bytes 2359296 | tf_op jit(solution)/shard_map/all_to_all | solution.py:14
  233.9 119.9 %all-to-all-start.1 = ((bf16[2,512,512]{2,1,0:T(8,128)(2,1)}), bf16[2,512,512]{2,1,0:T(8,128)(2,1)S(1)}, u32[]{:S(2)}, u32[]{:S(2)}) async-start(bf16[2,512,512]{2,1,0:T(8,128)(2,1)} %bitcast.108), calls=%async_computation.1 | async-start | bytes 2097152 | tf_op jit(solution)/shard_map/all_to_all | solution.py:38
  237.8 116.1 %copy-start.5 = (bf16[512,512]{1,0:T(8,128)(2,1)S(1)}, bf16[512,512]{1,0:T(8,128)(2,1)}, u32[]{:S(2)}) copy-start(bf16[512,512]{1,0:T(8,128)(2,1)} %param.14) | copy-start | bytes 1572868
  354.1 1.3 copy-start
  355.3 146.9 %all-to-all-start.2 = ((bf16[2,512,512]{1,2,0:T(8,128)(2,1)}), bf16[2,512,512]{1,2,0:T(8,128)(2,1)S(1)}, u32[]{:S(2)}, u32[]{:S(2)}) async-start(bf16[2,512,512]{1,2,0:T(8,128)(2,1)} %broadcast_in_dim.9), calls=%async_computation.2 | async-start | bytes 2097152 | tf_op jit(solution)/shard_map/all_to_all | solution.py:14
  359.1 124.9 %copy-start.7 = (bf16[2,512,576]{1,2,0:T(8,128)(2,1)S(1)}, bf16[2,512,576]{1,2,0:T(8,128)(2,1)}, u32[]{:S(2)}) copy-start(bf16[2,512,576]{1,2,0:T(8,128)(2,1)} %fusion.34) | copy-start | bytes 3538948
  499.0 1.4 copy-start.6
  500.4 19.2 %copy-start.10 = (bf16[2048,8]{0,1:T(8,128)(2,1)S(1)}, bf16[2048,8]{0,1:T(8,128)(2,1)}, u32[]{:S(2)}) copy-start(bf16[2048,8]{0,1:T(8,128)(2,1)} %param.21) | copy-start | bytes 98308
  522.0 11.2 %copy-start.4 = (bf16[512,576]{0,1:T(8,128)(2,1)S(1)}, bf16[512,576]{0,1:T(8,128)(2,1)}, u32[]{:S(2)}) copy-start(bf16[512,576]{0,1:T(8,128)(2,1)} %param.15) | copy-start | bytes 1769476
  522.0 111.0 %all-to-all-start.3 = ((bf16[128,2048,8]{1,2,0:T(8,128)(2,1)}), bf16[128,2048,8]{1,2,0:T(8,128)(2,1)}, u32[]{:S(2)}, u32[]{:S(2)}) async-start(bf16[128,2048,8]{1,2,0:T(8,128)(2,1)} %stack.4), calls=%async_computation.3 | async-start | bytes 8388608 | tf_op jit(solution)/shard_map/all_to_all | solution.py:87
  532.4 139.1 %all-gather.13.cloned.1.call-start = ((), (), s32[]{:S(2)}) async-start(), calls=%async_computation.12 | async-start | bytes 4227072 | tf_op jit(solution)/shard_map/all_gather | solution.py:82
  533.0 116.2 %copy-start.9 = (bf16[2152,9]{0,1:T(8,128)(2,1)S(1)}, bf16[2152,9]{0,1:T(8,128)(2,1)}, u32[]{:S(2)}) copy-start(bf16[2152,9]{0,1:T(8,128)(2,1)} %param.27) | copy-start | bytes 116212
  653.2 16.9 %copy-start.13 = (f32[1024]{0:T(1024)S(1)}, f32[1024]{0:T(1024)}, u32[]{:S(2)}) copy-start(f32[1024]{0:T(1024)} %param.19) | copy-start | bytes 12292
  653.2 237.1 %all-to-all-start.8 = ((bf16[128,2152,9]{1,2,0:T(8,128)(2,1)}), bf16[128,2152,9]{1,2,0:T(8,128)(2,1)}, u32[]{:S(2)}, u32[]{:S(2)}) async-start(bf16[128,2152,9]{1,2,0:T(8,128)(2,1)} %stack.5), calls=%async_computation.8 | async-start | bytes 17825792 | tf_op jit(solution)/shard_map/all_to_all | solution.py:87
  669.0 234.0 %all-gather.19.cloned.1.call-start = ((), (), s32[]{:S(2)}) async-start(), calls=%async_computation.15 | async-start | bytes 8982528 | tf_op jit(solution)/shard_map/all_gather | solution.py:82
  688.3 1.7 copy-start.11
  890.3 36.5 %all-to-all-start.4 = ((bf16[2,512,512]{2,1,0:T(8,128)(2,1)}), bf16[2,512,512]{2,1,0:T(8,128)(2,1)S(1)}, u32[]{:S(2)}, u32[]{:S(2)}) async-start(bf16[2,512,512]{2,1,0:T(8,128)(2,1)} %bitcast.106), calls=%async_computation.4 | async-start | bytes 2097152 | tf_op jit(solution)/shard_map/all_to_all | solution.py:38
  903.0 9.1 copy-start.8
  924.3 8.6 copy-start.1
  926.8 1.0 copy-start.2
  927.8 17.3 %all-to-all-start.9 = ((bf16[2,512,576]{1,2,0:T(8,128)(2,1)}), bf16[2,512,576]{1,2,0:T(8,128)(2,1)S(1)}, u32[]{:S(2)}, u32[]{:S(2)}) async-start(bf16[2,512,576]{1,2,0:T(8,128)(2,1)} %bitcast.29), calls=%async_computation.9 | async-start | bytes 2359296 | tf_op jit(solution)/shard_map/all_to_all | solution.py:38
Sparse Core Ops, SparseCore 0:
  11.8 114.9 all-gather.8
  130.6 100.2 all-gather.10
  234.4 115.1 all-gather.16
  353.2 119.4 all-gather.14
  536.5 130.3 all-gather.12
  673.1 181.9 all-gather.18
